TPU v7x, 32 devices: a whole 2x2x4 slice. The times are simulated.
32 devices in a mesh: x: 4 (over z), yz: 8 (over y, x, core).
Axes of the slice: x: 2, y: 2, z: 4, core: 2. Of those that a mesh axis runs over, the one named last changes fastest.
Arguments:
- x_in: bfloat16 [512, 2048], P(None, ('x', 'yz'))
- ln_scale: float32 [2048], P(('x', 'yz'))
- w_gate_up: bfloat16 [2048, 2, 8192], P('x', None, 'yz')
- w_attn: bfloat16 [2048, 2304], P('x', 'yz')
- w_down: bfloat16 [8192, 2048], P('yz', 'x')
- w_out: bfloat16 [2048, 2048], P('yz', 'x')
- k_cache: bfloat16 [512, 2048, 128], P(('x', 'yz'))
- v_cache: bfloat16 [512, 2048, 128], P(('x', 'yz'))
- lengths: int32 [512], P(('x', 'yz'))
- positions: int32 [512], P(('x', 'yz'))
Outputs:
- output 1: bfloat16 [512, 2048], P(None, ('x', 'yz'))
- output 2: bfloat16 [512, 2048, 128], P(('x', 'yz'))
- output 3: bfloat16 [512, 2048, 128], P(('x', 'yz'))
All inputs are finite; a program needn't handle non-finite values.
Results may differ from a plain program's by a relative error of at most 0.00344997.
Values are sent between devices in bfloat16 or wider.
A program may use at most 1 GiB of HBM per device.

v0:
```python
import jax
import jax.numpy as jnp
from jax import lax
from jax.sharding import PartitionSpec as P

LN_EPS = 1e-6
ROPE_BASE = 10000.0


def rotary(values, positions):
    half_dim = values.shape[-1] // 2
    inv_freq = ROPE_BASE ** (-jnp.arange(half_dim, dtype=jnp.float32) / half_dim)
    angles = positions.astype(jnp.float32)[:, None, None] * inv_freq
    cos_part = jnp.cos(angles)
    sin_part = jnp.sin(angles)
    lo_half = values[..., :half_dim]
    hi_half = values[..., half_dim:]
    return jnp.concatenate([lo_half * cos_part - hi_half * sin_part, hi_half * cos_part + lo_half * sin_part], axis=-1)


def solution(mesh):
    x_size = mesh.shape['x']
    yz_size = mesh.shape['yz']
    all_axes = ('x', 'yz')

    def local_step(x_in, ln_scale, w_gate_up, w_attn, w_down, w_out, k_cache, v_cache, lengths, positions):
        local_rows, seq_len, head_dim = k_cache.shape
        q_width = w_out.shape[0] * yz_size
        num_heads = q_width // head_dim
        d_model = x_in.shape[1] * x_size * yz_size
        x_float = x_in.astype(jnp.float32)
        ln_sums = jnp.stack([jnp.sum(x_float, axis=1), jnp.sum(x_float * x_float, axis=1)], axis=1)
        ln_sums = lax.psum(ln_sums, all_axes)
        mean_val = ln_sums[:, 0:1] / d_model
        var_val = ln_sums[:, 1:2] / d_model - mean_val * mean_val
        normed = ((x_float - mean_val) * lax.rsqrt(var_val + LN_EPS) * ln_scale).astype(jnp.bfloat16)
        h_rows = lax.all_gather(normed, 'yz', axis=1, tiled=True)
        gu_part = jnp.einsum('bd,dgf->bgf', h_rows, w_gate_up, preferred_element_type=jnp.float32)
        gate_up = lax.psum_scatter(gu_part, 'x', scatter_dimension=2, tiled=True).astype(jnp.bfloat16)
        hidden = (jax.nn.silu(gate_up[:, 0].astype(jnp.float32)) * gate_up[:, 1].astype(jnp.float32)).astype(jnp.bfloat16)
        hidden_rows = lax.all_gather(hidden, 'x', axis=1, tiled=True)
        proj_part = jnp.dot(h_rows, w_attn, preferred_element_type=jnp.float32)
        proj_rows = lax.psum_scatter(proj_part, 'x', scatter_dimension=0, tiled=True).astype(jnp.bfloat16)
        proj_local = lax.all_to_all(proj_rows, 'yz', 0, 1, tiled=True)
        q_raw = proj_local[:, :q_width].reshape(local_rows, num_heads, head_dim)
        k_tok = proj_local[:, q_width:q_width + head_dim]
        v_tok = proj_local[:, q_width + head_dim:]
        q_rot = rotary(q_raw.astype(jnp.float32), positions).astype(jnp.bfloat16)
        k_rot = rotary(k_tok[:, None, :].astype(jnp.float32), positions)[:, 0].astype(jnp.bfloat16)
        slot_ids = jnp.arange(seq_len)
        new_slot = (slot_ids[None, :] == lengths[:, None])[:, :, None]
        k_new = jnp.where(new_slot, k_rot[:, None, :], k_cache)
        v_new = jnp.where(new_slot, v_tok[:, None, :], v_cache)
        scores = jnp.einsum('bhd,bsd->bhs', q_rot, k_new, preferred_element_type=jnp.float32) * head_dim ** -0.5
        in_range = slot_ids[None, None, :] <= lengths[:, None, None]
        scores = jnp.where(in_range, scores, -1e30)
        prob_rows = jax.nn.softmax(scores, axis=-1).astype(jnp.bfloat16)
        attn_out = jnp.einsum('bhs,bsd->bhd', prob_rows, v_new, preferred_element_type=jnp.float32).astype(jnp.bfloat16)
        attn_out = attn_out.reshape(local_rows, q_width)
        o_rows = lax.all_to_all(attn_out, 'yz', 1, 0, tiled=True)
        o_all = lax.all_gather(o_rows, 'x', axis=0, tiled=True)
        mixed_sum = jnp.dot(hidden_rows, w_down, preferred_element_type=jnp.float32) + jnp.dot(o_all, w_out, preferred_element_type=jnp.float32)
        mixed_sum = lax.psum_scatter(mixed_sum, 'yz', scatter_dimension=1, tiled=True)
        y_out = (x_float + mixed_sum).astype(jnp.bfloat16)
        return y_out, k_new, v_new

    row_spec = P(None, all_axes)
    vec_spec = P(all_axes)
    cache_spec = P(all_axes, None, None)
    return jax.shard_map(
        local_step,
        mesh=mesh,
        in_specs=(row_spec, vec_spec, P('x', None, 'yz'), P('x', 'yz'), P('yz', 'x'), P('yz', 'x'), cache_spec, cache_spec, vec_spec, vec_spec),
        out_specs=(row_spec, cache_spec, cache_spec),
        check_vma=False,
    )
```

profile of v0, /device:TPU:0, one launch (start us, length us, event | category | flops | bytes accessed | tf_op | source)
XLA Modules:
  0.0 248.2 jit_solution(15313067434893292005)
XLA Ops:
  7.2 1.0 convert_reduce_fusion
  8.3 42.0 %psum.7 = f32[512,2]{0,1:T(2,128)S(1)} all-reduce(f32[512,2]{0,1:T(2,128)S(1)} %pad_maximum_fusion), channel_id=1, replica_groups=mesh['x'=4,'yz'=8] {'x','yz'}, use_global_device_ids=true, to_apply=%region_2.0 | all-reduce | flops 1024 | bytes 8192 | tf_op jit(solution)/shard_map/psum | solution.py:33
  50.3 0.9 fusion.16
  51.2 10.6 %all_gather.9 = bf16[512,512]{0,1:T(8,128)(2,1)S(1)} all-gather(bf16[512,64]{0,1:T(8,128)(2,1)S(1)} %fusion.16), channel_id=1, replica_groups=mesh['x'=4,'yz'=8] {'yz'}, dimensions={1}, use_global_device_ids=true | all-gather | bytes 589824 | tf_op jit(solution)/shard_map/all_gather | solution.py:37
  61.8 2.1 fusion.38
  64.0 3.4 %fusion.4 = f32[512,2,1024]{2,0,1:T(8,128)} fusion(bf16[512,2,1024]{2,1,0:T(2,128)(2,1)S(1)} %copy-done, bf16[512,512]{0,1:T(8,128)(2,1)S(1)} %all_gather.9), kind=kOutput, calls=%fused_computation.7 | convolution fusion | flops 1073741824 | bytes 6815744 | tf_op jit(solution)/shard_map/bd,dgf->bgf/dot_general | solution.py:38
  67.5 17.9 %reduce-scatter.6.cloned.1.call-done = f32[128,288]{0,1:T(8,128)} async-done(((f32[512,288]{0,1:T(8,128)}), f32[128,288]{0,1:T(8,128)}) %reduce-scatter.6.cloned.1.call-update) | async-done | bytes 147472 | tf_op jit(solution)/shard_map/reduce_scatter | solution.py:43
  85.4 0.9 convert_element_type.66
  86.4 0.8 copy.15
  87.1 3.6 %all-to-all-start = ((bf16[8,16,288]{2,1,0:T(8,128)(2,1)}), bf16[8,16,288]{2,1,0:T(8,128)(2,1)S(1)}, u32[]{:S(2)}, u32[]{:S(2)}) async-start(bf16[8,16,288]{2,1,0:T(8,128)(2,1)} %bitcast.8), calls=%async_computation.2 | async-start | bytes 196608 | tf_op jit(solution)/shard_map/all_to_all | solution.py:44
  90.9 4.8 %all-to-all-done = bf16[8,16,288]{2,1,0:T(8,128)(2,1)S(1)} async-done(((bf16[8,16,288]{2,1,0:T(8,128)(2,1)}), bf16[8,16,288]{2,1,0:T(8,128)(2,1)S(1)}, u32[]{:S(2)}, u32[]{:S(2)}) %all-to-all-start) | async-done | bytes 73760 | tf_op jit(solution)/shard_map/all_to_all | solution.py:44
  95.8 0.1 all_to_all.31
  96.3 11.9 %broadcast_select_fusion.1 = (bf16[16,2048,128]{2,1,0:T(8,128)(2,1)}, bf16[16,2048,128]{2,1,0:T(8,128)(2,1)}) fusion(bf16[16,2048,128]{2,1,0:T(8,128)(2,1)} %param.16, pred[16,2048]{1,0:T(8,128)(4,1)S(1)} %get-tuple-element.18, bf16[16,128]{1,0:T(8,128)(2,1)S(1)} %pad_maximum_fusion.1, bf16[16,2048,128]{2,1,0:T(8,128)(2,1)} %param.17, ...), kind=kLoop, calls=%fused_computation.2 | loop fusion | flops 8388608 | bytes 33595392 | tf_op jit(solution)/shard_map/jit(_where)/select_n | solution.py:52
  108.1 54.6 %reduce-scatter.4.cloned.1.call-done = f32[512,2,256]{2,0,1:T(8,128)} async-done(((f32[512,2,1024]{2,0,1:T(8,128)}), f32[512,2,256]{2,0,1:T(8,128)}) %reduce-scatter.4.cloned.1.call-update) | async-done | bytes 1048592 | tf_op jit(solution)/shard_map/reduce_scatter | solution.py:39
  162.7 1.3 convert_element_type.60
  164.0 0.9 fusion.12
  165.0 7.2 %fusion.34 = (f32[16,16]{1,0:T(8,128)S(1)}, f32[16,16,2048]{2,1,0:T(8,128)}) fusion(bf16[16,2048,128]{2,1,0:T(8,128)(2,1)} %get-tuple-element.9, pred[16,2048]{1,0:T(8,128)(4,1)S(1)} %get-tuple-element.17, bf16[16,16,64]{2,1,0:T(8,128)(2,1)S(1)} %get-tuple-element.6, bf16[16,16,64]{2,1,0:T(8,128)(2,1)S(1)} %get-tuple-element.5), kind=kOutput, calls=%fused_computation.64 | convolution fusion | flops 136448000 | bytes 10585088 | tf_op jit(solution)/shard_map/sub | solution.py:57
  172.1 5.3 %convolution_convert_fusion = bf16[16,16,128]{2,1,0:T(8,128)(2,1)S(1)} fusion(bf16[16,2048,128]{2,1,0:T(8,128)(2,1)} %get-tuple-element.10, f32[16,16,2048]{2,1,0:T(8,128)} %get-tuple-element.20, f32[16,16]{1,0:T(8,128)S(1)} %get-tuple-element.19), kind=kOutput, calls=%fused_computation.11 | convolution fusion | flops 135299072 | bytes 10552320 | tf_op jit(solution)/shard_map/bhs,bsd->bhd/dot_general | solution.py:58
  177.5 8.5 %all_to_all.38 = bf16[16,8,256]{2,0,1:T(8,128)(2,1)S(1)} all-to-all(bf16[16,8,256]{2,0,1:T(8,128)(2,1)S(1)} %copy.17), channel_id=1, replica_groups=mesh['x'=4,'yz'=8] {'yz'}, dimensions={1} | all-to-all | bytes 131072 | tf_op jit(solution)/shard_map/all_to_all | solution.py:60
  186.1 15.7 %all_gather.11 = bf16[512,256]{1,0:T(8,128)(2,1)S(1)} all-gather(bf16[128,256]{1,0:T(8,128)(2,1)S(1)} %bitcast.44), channel_id=1, replica_groups=mesh['x'=4,'yz'=8] {'x'}, dimensions={0}, use_global_device_ids=true | all-gather | bytes 327680 | tf_op jit(solution)/shard_map/all_gather | solution.py:61
  201.7 0.3 fusion.37
  202.1 3.3 %convolution_add_fusion = f32[512,512]{0,1:T(8,128)} fusion(f32[512,512]{0,1:T(8,128)S(1)} %fusion.37, bf16[512,1024]{1,0:T(8,128)(2,1)} %all-gather.2.cloned.1.call-done, bf16[1024,512]{1,0:T(8,128)(2,1)} %param.14), kind=kOutput, calls=%fused_computation.10 | convolution fusion | flops 537133056 | bytes 4194304 | tf_op jit(solution)/shard_map/dot_general | solution.py:62
  205.4 34.7 %reduce-scatter.8.cloned.1.call-done = f32[512,64]{0,1:T(8,128)} async-done(((f32[512,512]{0,1:T(8,128)}), f32[512,64]{0,1:T(8,128)}) %reduce-scatter.8.cloned.1.call-update) | async-done | bytes 131088 | tf_op jit(solution)/shard_map/reduce_scatter | solution.py:63
  240.1 1.5 fusion.17
  (34 shorter events, 0.9 us)
Async XLA Ops:
  7.2 56.8 %copy-start = (bf16[512,2,1024]{2,1,0:T(2,128)(2,1)S(1)}, bf16[512,2,1024]{2,1,0:T(2,128)(2,1)}, u32[]{:S(2)}) copy-start(bf16[512,2,1024]{2,1,0:T(2,128)(2,1)} %param.12) | copy-start | bytes 6291460
  7.2 78.3 %reduce-scatter.6.cloned.1.call-start = ((), (), s32[]{:S(2)}) async-start(), calls=%async_computation.7 | async-start | bytes 737280 | tf_op jit(solution)/shard_map/reduce_scatter | solution.py:43
  63.9 3.5 %copy-start.4 = (s32[16]{0:T(128)S(1)}, s32[16]{0:T(128)}, u32[]{:S(2)}) copy-start(s32[16]{0:T(128)} %param.19) | copy-start | bytes 196
  63.9 3.5 %copy-start.3 = (s32[16]{0:T(128)S(1)}, s32[16]{0:T(128)}, u32[]{:S(2)}) copy-start(s32[16]{0:T(128)} %param.18) | copy-start | bytes 196
  63.9 98.8 %reduce-scatter.4.cloned.1.call-start = ((), (), s32[]{:S(2)}) async-start(), calls=%async_computation.5 | async-start | bytes 5242880 | tf_op jit(solution)/shard_map/reduce_scatter | solution.py:39
  87.1 8.6 %all-to-all-start = ((bf16[8,16,288]{2,1,0:T(8,128)(2,1)}), bf16[8,16,288]{2,1,0:T(8,128)(2,1)S(1)}, u32[]{:S(2)}, u32[]{:S(2)}) async-start(bf16[8,16,288]{2,1,0:T(8,128)(2,1)} %bitcast.8), calls=%async_computation.2 | async-start | bytes 196608 | tf_op jit(solution)/shard_map/all_to_all | solution.py:44
  90.8 111.3 %all-gather.2.cloned.1.call-start = ((), (), s32[]{:S(2)}) async-start(), calls=%async_computation.6 | async-start | bytes 1310720 | tf_op jit(solution)/shard_map/all_gather | solution.py:41
  164.9 75.1 %reduce-scatter.8.cloned.1.call-start = ((), (), s32[]{:S(2)}) async-start(), calls=%async_computation.8 | async-start | bytes 1179648 | tf_op jit(solution)/shard_map/reduce_scatter | solution.py:63
  172.1 29.6 %copy-start.2 = (bf16[256,512]{1,0:T(8,128)(2,1)S(1)}, bf16[256,512]{1,0:T(8,128)(2,1)}, u32[]{:S(2)}) copy-start(bf16[256,512]{1,0:T(8,128)(2,1)} %param.15) | copy-start | bytes 786436
  177.5 62.6 %copy-start.1 = (bf16[512,64]{0,1:T(8,128)(2,1)S(1)}, bf16[512,64]{0,1:T(8,128)(2,1)}, u32[]{:S(2)}) copy-start(bf16[512,64]{0,1:T(8,128)(2,1)} %param.10) | copy-start | bytes 196612
Sparse Core Ops, SparseCore 0:
  64.0 21.3 reduce-scatter.5
  87.7 74.9 reduce-scatter.3
  165.0 34.5 all-gather.1
  205.5 34.5 reduce-scatter.7
where the time goes:
time: 249 us; the launch traced here: 248 us
  waiting for transfers between devices  112 us (45%)
  blocking collectives  76.8 us (31%)
  matrix products  21.5 us (9%)
  other arithmetic  19 us (8%)
  between operations  13.9 us (6%)
  starting transfers between devices  3.79 us (2%)
    reduce_scatter x1, waiting for transfers between devices, local_step(): lax.psum_scatter(gu_part, 'x', scatter_dimension=2, tiled=True)  54.6 us
    psum x1, blocking collectives, local_step(): ln_sums = lax.psum(ln_sums, all_axes)  42 us
    reduce_scatter x1, waiting for transfers between devices, local_step(): lax.psum_scatter(mixed_sum, 'yz', scatter_dimension=1, tiled=True)  34.7 us
    reduce_scatter x1, waiting for transfers between devices, local_step(): lax.psum_scatter(proj_part, 'x', scatter_dimension=0, tiled=True)  17.9 us
    all_gather x1, blocking collectives, local_step(): o_all = lax.all_gather(o_rows, 'x', axis=0, tiled=True)  15.7 us
    select_n x1, other arithmetic, local_step(): k_new = jnp.where(new_slot, k_rot[:, None, :], k_cache)  11.9 us
    all_gather x1, blocking collectives, local_step(): h_rows = lax.all_gather(normed, 'yz', axis=1, tiled=True)  10.6 us
    all_to_all x1, blocking collectives, local_step(): o_rows = lax.all_to_all(attn_out, 'yz', 1, 0, tiled=True)  8.53 us
  transfers between devices with their start and end apart: 5, of which 4 were waited for; matrix products, arithmetic and copies ran while one was open for 12% of the time, Pallas kernels for 0%

commit v1 on v0

v1 whole, which is shorter than its diff:
```python
import functools

import jax
import jax.numpy as jnp
from jax import lax
from jax.experimental import pallas as pl
from jax.experimental.pallas import tpu as pltpu
from jax.sharding import PartitionSpec as P

LN_EPS = 1e-6
ROPE_BASE = 10000.0
MESH = pl.DeviceIdType.MESH
F32 = jnp.float32
BF16 = jnp.bfloat16

NZ = 4
NP = 8


def rotary(values, positions):
    half_dim = values.shape[-1] // 2
    inv_freq = ROPE_BASE ** (-jnp.arange(half_dim, dtype=jnp.float32) / half_dim)
    angles = positions.astype(jnp.float32)[:, None, None] * inv_freq
    cos_part = jnp.cos(angles)
    sin_part = jnp.sin(angles)
    lo_half = values[..., :half_dim]
    hi_half = values[..., half_dim:]
    return jnp.concatenate([lo_half * cos_part - hi_half * sin_part, hi_half * cos_part + lo_half * sin_part], axis=-1)


def coords():
    z = lax.axis_index('x')
    p = lax.axis_index('yz')
    core = p % 2
    xx = (p // 2) % 2
    y = p // 4
    partner = p + 1 - 2 * core
    xn = p + 2 - 4 * xx
    yn = p + 4 - 8 * y
    diag = xn + 4 - 8 * y
    z1 = z % 2
    z2 = z // 2
    zs = [z, 2 * z2 + 1 - z1, 2 * (1 - z2) + z1, 3 - z]
    return z, p, core, partner, xn, yn, diag, zs


def entry_barrier(z, p, zs):
    sem = pltpu.get_barrier_semaphore()
    for k in range(1, NZ):
        pl.semaphore_signal(sem, inc=1, device_id=(zs[k], p), device_id_type=MESH)
    for k in range(1, NP):
        pl.semaphore_signal(sem, inc=1, device_id=(z, (p + k) % NP), device_id_type=MESH)
    pl.semaphore_wait(sem, NZ - 1 + NP - 1)


def rcopy(src, dst, send, recv, dev):
    return pltpu.make_async_remote_copy(src_ref=src, dst_ref=dst, send_sem=send, recv_sem=recv, device_id=dev, device_id_type=MESH)


def kernel_a(xT_ref, ln_ref, wattn_ref, hT_ref, qkv_ref,
             xg, lng, zsend, zrecv, zq, s1, s2,
             xsend, xrecv, lsend, lrecv, zsend_sem, zrecv_sem, qsend, qrecv):
    z, p, core, partner, xn, yn, diag, zs = coords()
    xg[z, p] = xT_ref[...]
    lng[z, p] = ln_ref[...]
    entry_barrier(z, p, zs)
    sends = []

    def send(sem_i, src_z, src_p, dev):
        c = rcopy(xg.at[src_z, src_p], xg.at[src_z, src_p], xsend.at[sem_i], xrecv.at[src_z, src_p], dev)
        c.start()
        sends.append(c)

    def lsendf(sem_i, src_z, src_p, dev):
        c = rcopy(lng.at[src_z, src_p], lng.at[src_z, src_p], lsend.at[sem_i], lrecv.at[src_z, src_p], dev)
        c.start()
        sends.append(c)

    def wait_x(src_z, src_p):
        rcopy(xg.at[src_z, src_p], xg.at[src_z, src_p], xsend.at[0], xrecv.at[src_z, src_p], (z, p)).wait_recv()

    def wait_l(src_z, src_p):
        rcopy(lng.at[src_z, src_p], lng.at[src_z, src_p], lsend.at[0], lrecv.at[src_z, src_p], (z, p)).wait_recv()

    n = 0
    ln = 0
    for k in (3, 2, 1):
        lsendf(ln, z, p, (zs[k], p))
        send(n, z, p, (zs[k], p))
        n += 1
        ln += 1
    for k in range(NZ):
        if k:
            wait_x(zs[k], p)
            wait_l(zs[k], p)
        for dev in (xn, yn, partner):
            send(n, zs[k], p, (z, dev))
            n += 1
        for j in range(1, NP):
            lsendf(ln, zs[k], p, (z, (p + j) % NP))
            ln += 1
    for k in range(NZ):
        wait_x(zs[k], xn)
        if k < 2:
            send(n, zs[k], xn, (z, yn))
            n += 1
        send(n, zs[k], xn, (z, partner))
        n += 1
        wait_x(zs[k], yn)
        if k >= 2:
            send(n, zs[k], yn, (z, xn))
            n += 1
        send(n, zs[k], yn, (z, partner))
        n += 1
    for k in range(NZ):
        wait_x(zs[k], diag)
        send(n, zs[k], diag, (z, partner))
        n += 1
    pd = [partner + xn - p, partner + yn - p, partner + diag - p]
    for k in range(NZ):
        wait_x(zs[k], partner)
    for k in range(NZ):
        for q in pd:
            wait_x(zs[k], q)
    for k in range(NZ):
        for j in range(1, NP):
            wait_l(zs[k], (p + j) % NP)

    s1[...] = jnp.zeros_like(s1)
    s2[...] = jnp.zeros_like(s2)

    def stat(i, carry):
        blk = xg[i // NP, i % NP].astype(F32).reshape(8, 8, 512)
        s1[...] += jnp.sum(blk, axis=0)
        s2[...] += jnp.sum(blk * blk, axis=0)
        return carry

    lax.fori_loop(0, NZ * NP, stat, 0)
    mean = jnp.sum(s1[...], axis=0, keepdims=True) / 2048.0
    var = jnp.sum(s2[...], axis=0, keepdims=True) / 2048.0 - mean * mean
    rstd = lax.rsqrt(var + LN_EPS)
    lnT = jnp.concatenate([lng[i // NP, i % NP, 0:1, :] for i in range(32)] + [jnp.zeros((96, 128), F32)], axis=0).T
    for i in range(NZ * NP):
        sc = lnT[0:64, i:i + 1]
        hT_ref[i * 64:(i + 1) * 64, :] = ((xg[i // NP, i % NP].astype(F32) - mean) * rstd * sc).astype(BF16)

    h_mine = hT_ref[pl.ds(pl.multiple_of(z * 512, 512), 512), :]
    part = jnp.dot(wattn_ref[...], h_mine, preferred_element_type=F32)
    for q in range(NZ):
        zsend[q] = part[:, q * 128:(q + 1) * 128]
    for k in (3, 2, 1):
        c = rcopy(zsend.at[zs[k]], zrecv.at[z], zsend_sem.at[k], zrecv_sem.at[z], (zs[k], p))
        c.start()
        sends.append(c)
    for k in range(1, NZ):
        rcopy(zsend.at[0], zrecv.at[zs[k]], zsend_sem.at[0], zrecv_sem.at[zs[k]], (z, p)).wait_recv()
    zrecv[z] = zsend[z]
    zt = zrecv[0] + zrecv[1] + zrecv[2] + zrecv[3]
    ztt = zt.T.astype(BF16)
    zq[...] = ztt.reshape(NP, 16, 288)
    for j in range(1, NP):
        q = (p + j) % NP
        c = rcopy(zq.at[q], qkv_ref.at[p], qsend.at[j], qrecv.at[p], (z, q))
        c.start()
        sends.append(c)
    qkv_ref[p] = zq[p]
    for j in range(1, NP):
        q = (p + j) % NP
        rcopy(zq.at[0], qkv_ref.at[q], qsend.at[0], qrecv.at[q], (z, p)).wait_recv()
    for c in sends:
        c.wait_send()


def call_a(xT, lnb, wattnT):
    vm = pl.BlockSpec(memory_space=pltpu.VMEM)
    return pl.pallas_call(
        kernel_a,
        out_shape=(jax.ShapeDtypeStruct((2048, 512), BF16), jax.ShapeDtypeStruct((NP, 16, 288), BF16)),
        in_specs=[vm] * 3,
        out_specs=(vm, vm),
        scratch_shapes=[
            pltpu.VMEM((NZ, NP, 64, 512), BF16),
            pltpu.VMEM((NZ, NP, 8, 128), F32),
            pltpu.VMEM((NZ, 288, 128), F32),
            pltpu.VMEM((NZ, 288, 128), F32),
            pltpu.VMEM((NP, 16, 288), BF16),
            pltpu.VMEM((8, 512), F32),
            pltpu.VMEM((8, 512), F32),
            pltpu.SemaphoreType.DMA((40,)),
            pltpu.SemaphoreType.DMA((NZ, NP)),
            pltpu.SemaphoreType.DMA((40,)),
            pltpu.SemaphoreType.DMA((NZ, NP)),
            pltpu.SemaphoreType.DMA((NZ,)),
            pltpu.SemaphoreType.DMA((NZ,)),
            pltpu.SemaphoreType.DMA((NP,)),
            pltpu.SemaphoreType.DMA((NP,)),
        ],
        compiler_params=pltpu.CompilerParams(collective_id=0, has_side_effects=True, vmem_limit_bytes=32 * 1024 * 1024),
        name='gather_norm_qkv',
    )(xT, lnb, wattnT)


def kernel_b(len_ref, q_ref, k_ref, v_ref, kc_ref, vc_ref, o_ref, kn_ref, vn_ref):
    b = pl.program_id(0)
    length = len_ref[b]
    kn_ref[...] = kc_ref[...]
    vn_ref[...] = vc_ref[...]
    base = pl.multiple_of((length // 16) * 16, 16)
    rows = base + lax.broadcasted_iota(jnp.int32, (16, 128), 0)
    hit = rows == length
    kn_ref[0, pl.ds(base, 16), :] = jnp.where(hit, k_ref[0].astype(F32), kc_ref[0, pl.ds(base, 16), :].astype(F32)).astype(BF16)
    vn_ref[0, pl.ds(base, 16), :] = jnp.where(hit, v_ref[0].astype(F32), vc_ref[0, pl.ds(base, 16), :].astype(F32)).astype(BF16)
    scores = lax.dot_general(q_ref[0], kn_ref[0], (((1,), (1,)), ((), ())), preferred_element_type=F32) * (128.0 ** -0.5)
    slot = lax.broadcasted_iota(jnp.int32, scores.shape, 1)
    scores = jnp.where(slot <= length, scores, -1e30)
    top = jnp.max(scores, axis=1, keepdims=True)
    e = jnp.exp(scores - top)
    probs = (e / jnp.sum(e, axis=1, keepdims=True)).astype(BF16)
    o_ref[0] = jnp.dot(probs, vn_ref[0], preferred_element_type=F32).astype(BF16)


def call_b(lengths, q_rot, k_rot, v_tok, k_cache, v_cache):
    rows, seq, hd = k_cache.shape
    heads = q_rot.shape[1]
    blk = lambda *s: pl.BlockSpec((1,) + s, lambda i, *_: (i, 0, 0))
    return pl.pallas_call(
        kernel_b,
        grid_spec=pltpu.PrefetchScalarGridSpec(
            num_scalar_prefetch=1,
            grid=(rows,),
            in_specs=[blk(heads, hd), blk(1, hd), blk(1, hd), blk(seq, hd), blk(seq, hd)],
            out_specs=(blk(heads, hd), blk(seq, hd), blk(seq, hd)),
        ),
        out_shape=(
            jax.ShapeDtypeStruct((rows, heads, hd), BF16),
            jax.ShapeDtypeStruct(k_cache.shape, BF16),
            jax.ShapeDtypeStruct(v_cache.shape, BF16),
        ),
        compiler_params=pltpu.CompilerParams(vmem_limit_bytes=60 * 1024 * 1024),
        cost_estimate=pl.CostEstimate(flops=12_000_000_000, bytes_accessed=33_000_000, transcendentals=0),
        name='attend',
    )(lengths, q_rot, k_rot, v_tok, k_cache, v_cache)


def kernel_c(hT_ref, w0_ref, w1_ref, w2_ref, w3_ref, wd_ref, wo_ref, o_ref, xT_ref, y_ref,
             wdT, woT, og, hid, ysum, r1, r2, acc4,
             osend, orecv, gsend, grecv, hsend, hrecv, r1send, r1recv, r2send, r2recv):
    z, p, core, partner, xn, yn, diag, zs = coords()
    entry_barrier(z, p, zs)
    sends = []
    for j in range(1, NP):
        q = (p + j) % NP
        c = rcopy(o_ref.at[q], og.at[z, p], osend.at[j], orecv.at[p], (z, q))
        c.start()
        sends.append(c)
    og[z, p] = o_ref[p]
    g = None
    for i, w_ref in enumerate((w0_ref, w1_ref, w2_ref, w3_ref)):
        src = (z + NZ - i) % NZ
        h_blk = hT_ref[pl.ds(pl.multiple_of(src * 512, 512), 512), :]
        t = jnp.dot(w_ref[...], h_blk, preferred_element_type=F32)
        g = t if g is None else g + t
    gate = g[0:256].astype(BF16).astype(F32)
    up = g[256:512].astype(BF16).astype(F32)
    hid[z] = (jax.nn.silu(gate) * up).astype(BF16)

    def fwd(sem, src, dev):
        c = rcopy(hid.at[src], hid.at[src], hsend.at[sem], hrecv.at[src], dev)
        c.start()

    def fwd_wait_send(sem):
        rcopy(hid.at[0], hid.at[0], hsend.at[sem], hrecv.at[0], (z, p)).wait_send()

    def wait_hid(src):
        rcopy(hid.at[0], hid.at[src], hsend.at[0], hrecv.at[src], (z, p)).wait_recv()

    @pl.when(z < 3)
    def _():
        fwd(0, z, (z + 1, p))

    @pl.when(z > 0)
    def _():
        fwd(1, z, (z - 1, p))

    for j in range(1, NP):
        q = (p + j) % NP
        rcopy(o_ref.at[0], og.at[z, q], osend.at[0], orecv.at[q], (z, p)).wait_recv()
    for k in (3, 2, 1):
        c = rcopy(og.at[z], og.at[z], gsend.at[k], grecv.at[z], (zs[k], p))
        c.start()
        sends.append(c)
    wdT[...] = wd_ref[...].T
    woT[...] = wo_ref[...].T

    for k in range(1, NZ):
        @pl.when(z >= k)
        def _():
            wait_hid(z - k)

            @pl.when(z < 3)
            def _():
                fwd(2 * k, z - k, (z + 1, p))

        @pl.when(z + k <= 3)
        def _():
            wait_hid(z + k)

            @pl.when(z > 0)
            def _():
                fwd(2 * k + 1, z + k, (z - 1, p))

    for k in range(1, NZ):
        rcopy(og.at[0], og.at[zs[k]], gsend.at[0], grecv.at[zs[k]], (z, p)).wait_recv()

    hid_all = hid[...].reshape(1024, 512)
    o_all = og[...].reshape(512, 256)
    yt = jnp.dot(wdT[...], hid_all, preferred_element_type=F32)
    yt = yt + lax.dot_general(woT[...], o_all, (((1,), (1,)), ((), ())), preferred_element_type=F32)
    ysum[...] = yt.reshape(NP, 64, 512)
    for i in range(4):
        c = rcopy(ysum.at[2 * i + 1 - core], r1.at[i], r1send.at[i], r1recv.at[i], (z, partner))
        c.start()
        sends.append(c)
    chip = p // 2
    others = [xn // 2, yn // 2, diag // 2]
    for i, (t, dev) in enumerate(zip(others, (xn, yn, diag))):
        rcopy(ysum.at[0], r1.at[t], r1send.at[0], r1recv.at[t], (z, p)).wait_recv()
        acc4[i] = ysum[2 * t + core] + r1[t]
        c = rcopy(acc4.at[i], r2.at[i], r2send.at[i], r2recv.at[i], (z, dev))
        c.start()
        sends.append(c)
    rcopy(ysum.at[0], r1.at[chip], r1send.at[0], r1recv.at[chip], (z, p)).wait_recv()
    mine = ysum[p] + r1[chip]
    for i in range(3):
        rcopy(acc4.at[0], r2.at[i], r2send.at[0], r2recv.at[i], (z, p)).wait_recv()
        mine = mine + r2[i]
    y_ref[...] = (xT_ref[...].astype(F32) + mine).astype(BF16)
    for c in sends:
        c.wait_send()

    for k in range(NZ):
        @pl.when((z >= k) & (z < 3))
        def _():
            fwd_wait_send(2 * k)

        @pl.when((z + k <= 3) & (z > 0))
        def _():
            fwd_wait_send(2 * k + 1)


def call_c(hT, ws, wd, wo, o8, xT):
    vm = pl.BlockSpec(memory_space=pltpu.VMEM)
    return pl.pallas_call(
        kernel_c,
        out_shape=jax.ShapeDtypeStruct((64, 512), BF16),
        in_specs=[vm] * 9,
        out_specs=vm,
        scratch_shapes=[
            pltpu.VMEM((512, 1024), BF16),
            pltpu.VMEM((512, 256), BF16),
            pltpu.VMEM((NZ, NP, 16, 256), BF16),
            pltpu.VMEM((NZ, 256, 512), BF16),
            pltpu.VMEM((NP, 64, 512), F32),
            pltpu.VMEM((4, 64, 512), F32),
            pltpu.VMEM((3, 64, 512), F32),
            pltpu.VMEM((3, 64, 512), F32),
            pltpu.SemaphoreType.DMA((NP,)),
            pltpu.SemaphoreType.DMA((NP,)),
            pltpu.SemaphoreType.DMA((NZ,)),
            pltpu.SemaphoreType.DMA((NZ,)),
            pltpu.SemaphoreType.DMA((8,)),
            pltpu.SemaphoreType.DMA((NZ,)),
            pltpu.SemaphoreType.DMA((4,)),
            pltpu.SemaphoreType.DMA((4,)),
            pltpu.SemaphoreType.DMA((3,)),
            pltpu.SemaphoreType.DMA((3,)),
        ],
        compiler_params=pltpu.CompilerParams(collective_id=1, has_side_effects=True, vmem_limit_bytes=48 * 1024 * 1024),
        cost_estimate=pl.CostEstimate(flops=12_000_000_000, bytes_accessed=6_000_000, transcendentals=0),
        name='mlp_out',
    )(hT, *ws, wd, wo, o8, xT)


def solution(mesh):
    all_axes = ('x', 'yz')

    def local_step(x_in, ln_scale, w_gate_up, w_attn, w_down, w_out, k_cache, v_cache, lengths, positions):
        z = lax.axis_index('x')
        xT = x_in.T
        wattnT = w_attn.T
        lnb = jnp.broadcast_to(jnp.pad(ln_scale, (0, 64))[None, :], (8, 128))
        w4 = jnp.transpose(w_gate_up.reshape(512, 2, NZ, 256), (2, 1, 3, 0)).reshape(NZ, 512, 512)
        hT, qkv = call_a(xT, lnb, wattnT)
        w4, hT, qkv = lax.optimization_barrier((w4, hT, qkv))
        ws = [lax.dynamic_index_in_dim(w4, z, 0, keepdims=False)]
        for s in range(1, NZ):
            piece = lax.dynamic_index_in_dim(w4, (z + s) % NZ, 0, keepdims=False)
            ws.append(lax.ppermute(piece, 'x', [(i, (i + s) % NZ) for i in range(NZ)]))
        proj = jnp.transpose(qkv, (1, 0, 2)).reshape(16, 2304)
        q_raw = proj[:, :2048].reshape(16, 16, 128)
        k_tok = proj[:, 2048:2176]
        v_tok = proj[:, 2176:]
        q_rot = rotary(q_raw.astype(F32), positions).astype(BF16)
        k_rot = rotary(k_tok[:, None, :].astype(F32), positions).astype(BF16)
        o, k_new, v_new = call_b(lengths, q_rot, k_rot, v_tok[:, None, :], k_cache, v_cache)
        o8 = jnp.transpose(o.reshape(16, NP, 256), (1, 0, 2))
        yT = call_c(hT, ws, w_down, w_out, o8, xT)
        return yT.T, k_new, v_new

    row_spec = P(None, all_axes)
    vec_spec = P(all_axes)
    cache_spec = P(all_axes, None, None)
    return jax.shard_map(
        local_step,
        mesh=mesh,
        in_specs=(row_spec, vec_spec, P('x', None, 'yz'), P('x', 'yz'), P('yz', 'x'), P('yz', 'x'), cache_spec, cache_spec, vec_spec, vec_spec),
        out_specs=(row_spec, cache_spec, cache_spec),
        check_vma=False,
    )
```

time: 249 us -> 145 us (0.58)
  Pallas kernels: 0 us -> 106 us
  waiting for transfers between devices: 112 us -> 19.6 us
  blocking collectives: 76.8 us -> 0 us
  matrix products: 21.5 us -> 0 us
  other arithmetic: 19 us -> 1.92 us
  between operations: 13.9 us -> 0.85 us
  local copies, waits for them, and re-layouts: 1 us -> 13.4 us
    reduce_scatter x3 -> x0, waiting for transfers between devices: 107 us -> none  [the longest x1 54.6 us: local_step(): lax.psum_scatter(gu_part, 'x', scatter_dimension=2, tiled=True)]
    pallas_call x0 -> x3, Pallas kernels: none -> 106 us  [the longest x1 44.9 us: call_a(): pl.pallas_call(kernel_a, out_shape=(jax.ShapeDtypeStruct((2048, 512), BF1...]
    psum x1 -> x0, blocking collectives: 42 us -> none  [local_step(): ln_sums = lax.psum(ln_sums, all_axes)]
    all_gather x2 -> x0, blocking collectives: 26.3 us -> none  [the longest x1 15.7 us: local_step(): o_all = lax.all_gather(o_rows, 'x', axis=0, tiled=True)]
    ppermute x0 -> x3, waiting for transfers between devices: none -> 19.6 us  [local_step(): ws.append(lax.ppermute(piece, 'x', [(i, (i + s) % NZ) for i in range(NZ)]))]
    dot_general x5 -> x0, matrix products: 14.4 us -> none  [the longest x1 5.32 us: local_step(): jnp.einsum('bhs,bsd->bhd', prob_rows, v_new, preferred_element_type=jnp.f...]
    select_n x1 -> x0, other arithmetic: 11.9 us -> none  [local_step(): k_new = jnp.where(new_slot, k_rot[:, None, :], k_cache)]
    all_to_all x1 -> x0, blocking collectives: 8.53 us -> none  [local_step(): o_rows = lax.all_to_all(attn_out, 'yz', 1, 0, tiled=True)]
  transfers between devices with their start and end apart: 5 -> 3, of which waited for: 4 -> 1; matrix products, arithmetic and copies ran while one was open for 12% -> 3% of each run, Pallas kernels for 0% -> 14%
where the time goes in v1:
time: 145 us; the launch traced here: 144 us
  Pallas kernels  106 us (73%)
  waiting for transfers between devices  19.6 us (14%)
  local copies, waits for them, and re-layouts  13.4 us (9%)
  starting transfers between devices  2.03 us (1%)
  other arithmetic  1.92 us (1%)
    pallas_call x1, Pallas kernels, call_a(): pl.pallas_call(kernel_a, out_shape=(jax.ShapeDtypeStruct((2048, 512), BF1...  44.9 us
    pallas_call x1, Pallas kernels, call_c(): pl.pallas_call(kernel_c, out_shape=jax.ShapeDtypeStruct((64, 512), BF16),...  41.6 us
    pallas_call x1, Pallas kernels, call_b(): pl.pallas_call(kernel_b, grid_spec=pltpu.PrefetchScalarGridSpec(num_scala...  19.7 us
    ppermute x3, waiting for transfers between devices, local_step(): ws.append(lax.ppermute(piece, 'x', [(i, (i + s) % NZ) for i in range(NZ)]))  19.6 us
    reshape x1, local copies, waits for them, and re-layouts, local_step(): w_gate_up.reshape(512, 2, NZ, 256)  3.15 us
    transpose x1, local copies, waits for them, and re-layouts, local_step(): jnp.transpose(w_gate_up.reshape(512, 2, NZ, 256), (2, 1, 3, 0))  3 us
  transfers between devices with their start and end apart: 3, of which 1 were waited for; matrix products, arithmetic and copies ran while one was open for 3% of the time, Pallas kernels for 14%

profile of v1, /device:TPU:0, one launch (start us, length us, event | category | flops | bytes accessed | tf_op | source)
XLA Modules:
  0.0 143.9 jit_solution(1689221301470938525)
XLA Ops:
  0.7 3.2 %reshape.158 = bf16[512,2,4,256]{3,2,1,0:T(4,128)(2,1)S(1)} reshape(bf16[512,2,1024]{2,1,0:T(2,128)(2,1)} %param.12) | data formatting | bytes 4194304 | tf_op jit(solution)/shard_map/reshape | solution.py:392
  3.8 0.0 copy-start.4
  3.8 0.0 copy-start
  3.9 0.0 copy-start.1
  3.9 3.0 %copy.20 = bf16[4,2,256,512]{3,2,1,0:T(8,128)(2,1)} copy(bf16[4,2,256,512]{2,0,1,3:T(4,128)(2,1)S(1)} %bitcast.31) | data formatting | bytes 4194304 | tf_op jit(solution)/shard_map/transpose | solution.py:392
  6.9 44.9 %gather_norm_qkv.1 = (bf16[2048,512]{1,0:T(8,128)(2,1)S(1)}, bf16[8,16,288]{2,1,0:T(8,128)(2,1)S(1)}) custom-call(bf16[64,512]{1,0:T(8,128)(2,1)S(1)} %bitcast.28, f32[8,128]{1,0:T(8,128)S(1)} %broadcast_in_dim.4.ln_ref, bf16[288,512]{1,0:T(8,128)(2,1)S(1)} %bitcast.24), custom_call_target="tpu_custom_call" | custom-call | tf_op jit(solution)/shard_map/gather_norm_qkv/pallas_call | solution.py:176
  51.8 2.7 %dynamic-slice_bitcast_fusion = (bf16[512,512]{1,0:T(8,128)(2,1)}, bf16[512,512]{1,0:T(8,128)(2,1)}, bf16[512,512]{1,0:T(8,128)(2,1)}, bf16[512,512]{1,0:T(8,128)(2,1)S(1)}) fusion(bf16[4,512,512]{2,1,0:T(8,128)(2,1)} %bitcast.30, s32[]{:T(128)S(6)} %select_n.34, s32[]{:T(128)S(6)} %select_n.32, s32[]{:T(128)S(6)} %select_n.30, s32[]{:T(128)S(6)} %select_n.28), kind=kLoop, calls=%fused_computation | loop fusion | bytes 4194320 | tf_op jit(solution)/shard_map/jit(dynamic_index_in_dim)/squeeze | solution.py:397
  54.5 1.4 collective-permute-start.2
  55.9 0.7 collective-permute-start
  56.6 0.1 reshape.160
  56.8 0.6 copy.23.v_ref
  57.4 0.1 multiply_cosine_fusion
  57.5 0.1 mul.89
  57.6 0.3 subtract_convert_fusion.1
  57.8 0.7 pad_maximum_fusion.1.k_ref
  58.5 0.1 subtract_convert_fusion
  58.6 0.7 pad_maximum_fusion.q_ref
  59.4 19.7 %attend.1 = (bf16[16,16,128]{2,1,0:T(8,128)(2,1)}, bf16[16,2048,128]{2,1,0:T(8,128)(2,1)}, bf16[16,2048,128]{2,1,0:T(8,128)(2,1)}) custom-call(s32[16]{0:T(128)} %len_ref.1, bf16[16,16,128]{2,1,0:T(8,128)(2,1)} %pad_maximum_fusion.q_ref, bf16[16,1,128]{2,1,0:T(2,128)(2,1)} %pad_maximum_fusion.1.k_ref, bf16[16,1,128]{2,1,0:T(2,128)(2,1)} %copy.23.v_ref, ...), custom_call_target="tpu_custom_call" | custom-call | flops 12000000000 | bytes 33000000 | tf_op jit(solution)/shard_map/attend/pallas_call | solution.py:226
  79.0 0.9 reshape.161
  79.9 19.6 %collective-permute-done.1.w2_ref = bf16[512,512]{1,0:T(8,128)(2,1)} collective-permute-done((bf16[512,512]{1,0:T(8,128)(2,1)}, bf16[512,512]{1,0:T(8,128)(2,1)}, u32[]{:S(2)}, u32[]{:S(2)}) %collective-permute-start.1) | collective-permute-done | bytes 524320 | tf_op jit(solution)/shard_map/ppermute | solution.py:398
  99.5 1.2 copy-done.2
  100.7 0.9 copy-done.3
  101.7 41.6 %mlp_out.1 = bf16[64,512]{1,0:T(8,128)(2,1)S(1)} custom-call(bf16[2048,512]{1,0:T(8,128)(2,1)S(1)} %get-tuple-element.13.hT_ref, bf16[512,512]{1,0:T(8,128)(2,1)S(1)} %get-tuple-element.22.w0_ref, bf16[512,512]{1,0:T(8,128)(2,1)} %collective-permute-done.w1_ref, bf16[512,512]{1,0:T(8,128)(2,1)} %collective-permute-done.1.w2_ref, ...), custom_call_target="tpu_custom_call" | custom-call | flops 12000000000 | bytes 6000000 | tf_op jit(solution)/shard_map/mlp_out/pallas_call | solution.py:353
  143.3 0.6 copy.29
  (19 shorter events, 0.1 us)
Async XLA Ops:
  3.8 3.0 %copy-start.4 = (f32[64]{0:T(128)S(1)}, f32[64]{0:T(128)}, u32[]{:S(2)}) copy-start(f32[64]{0:T(128)} %param.11) | copy-start | bytes 772
  3.8 3.0 %copy-start = (bf16[512,288]{0,1:T(8,128)(2,1)S(1)}, bf16[512,288]{0,1:T(8,128)(2,1)}, u32[]{:S(2)}) copy-start(bf16[512,288]{0,1:T(8,128)(2,1)} %param.13) | copy-start | bytes 884740
  3.9 3.0 %copy-start.1 = (bf16[512,64]{0,1:T(8,128)(2,1)S(1)}, bf16[512,64]{0,1:T(8,128)(2,1)}, u32[]{:S(2)}) copy-start(bf16[512,64]{0,1:T(8,128)(2,1)} %param.10) | copy-start | bytes 196612
  51.8 4.9 %copy-start.5 = (s32[16]{0:T(128)S(1)}, s32[16]{0:T(128)}, u32[]{:S(2)}) copy-start(s32[16]{0:T(128)} %param.19) | copy-start | bytes 196
  54.5 25.4 %collective-permute-start.2 = (bf16[512,512]{1,0:T(8,128)(2,1)}, bf16[512,512]{1,0:T(8,128)(2,1)S(1)}, u32[]{:S(2)}, u32[]{:S(2)}) collective-permute-start(bf16[512,512]{1,0:T(8,128)(2,1)} %get-tuple-element.19), channel_id=1, source_target_pairs={{0,24},{8,0},{16,8},{24,16},{1,25},{9,1},{17,9},{25,17},{2,26},{10... | collective-permute-start | bytes 1572872 | tf_op jit(solution)/shard_map/ppermute | solution.py:398
  55.9 43.6 %collective-permute-start.1 = (bf16[512,512]{1,0:T(8,128)(2,1)}, bf16[512,512]{1,0:T(8,128)(2,1)}, u32[]{:S(2)}, u32[]{:S(2)}) collective-permute-start(bf16[512,512]{1,0:T(8,128)(2,1)} %get-tuple-element.20), channel_id=1, source_target_pairs={{0,16},{8,24},{16,0},{24,8},{1,17},{9,25},{17,1},{25,9},{2,18},{10... | collective-permute-start | bytes 1572872 | tf_op jit(solution)/shard_map/ppermute | solution.py:398
  55.9 43.6 %collective-permute-start = (bf16[512,512]{1,0:T(8,128)(2,1)}, bf16[512,512]{1,0:T(8,128)(2,1)}, u32[]{:S(2)}, u32[]{:S(2)}) collective-permute-start(bf16[512,512]{1,0:T(8,128)(2,1)} %get-tuple-element.21), channel_id=1, source_target_pairs={{0,8},{8,16},{16,24},{24,0},{1,9},{9,17},{17,25},{25,1},{2,10},{10... | collective-permute-start | bytes 1572872 | tf_op jit(solution)/shard_map/ppermute | solution.py:398
  99.5 1.2 copy-start.2
  100.7 0.9 copy-start.3

commit v2 on v1

v2 whole, which is shorter than its diff:
```python
import functools

import jax
import jax.numpy as jnp
from jax import lax
from jax.experimental import pallas as pl
from jax.experimental.pallas import tpu as pltpu
from jax.sharding import PartitionSpec as P

LN_EPS = 1e-6
ROPE_BASE = 10000.0
MESH = pl.DeviceIdType.MESH
F32 = jnp.float32
BF16 = jnp.bfloat16

NZ = 4
NP = 8
C1 = 64
C2 = 96
C3 = 96
CA = C1 + C2
CHUNKS = 4
LANES = 512 // CHUNKS


def rotary(values, positions):
    half_dim = values.shape[-1] // 2
    inv_freq = ROPE_BASE ** (-jnp.arange(half_dim, dtype=jnp.float32) / half_dim)
    angles = positions.astype(jnp.float32)[:, None, None] * inv_freq
    cos_part = jnp.cos(angles)
    sin_part = jnp.sin(angles)
    lo_half = values[..., :half_dim]
    hi_half = values[..., half_dim:]
    return jnp.concatenate([lo_half * cos_part - hi_half * sin_part, hi_half * cos_part + lo_half * sin_part], axis=-1)


def coords():
    z = lax.axis_index('x')
    p = lax.axis_index('yz')
    core = p % 2
    xx = (p // 2) % 2
    y = p // 4
    partner = p + 1 - 2 * core
    xn = p + 2 - 4 * xx
    yn = p + 4 - 8 * y
    diag = xn + 4 - 8 * y
    z1 = z % 2
    z2 = z // 2
    zs = [z, 2 * z2 + 1 - z1, 2 * (1 - z2) + z1, 3 - z]
    return z, p, core, partner, xn, yn, diag, zs


def entry_barrier(z, p, zs):
    sem = pltpu.get_barrier_semaphore()
    for k in range(1, NZ):
        pl.semaphore_signal(sem, inc=1, device_id=(zs[k], p), device_id_type=MESH)
    for k in range(1, NP):
        pl.semaphore_signal(sem, inc=1, device_id=(z, (p + k) % NP), device_id_type=MESH)
    pl.semaphore_wait(sem, NZ - 1 + NP - 1)


def rcopy(src, dst, send, recv, dev):
    return pltpu.make_async_remote_copy(src_ref=src, dst_ref=dst, send_sem=send, recv_sem=recv, device_id=dev, device_id_type=MESH)


def attn_start(q):
    return pl.multiple_of(64 * q + 16 * (q // 2), 16)


def kernel_a(xT_ref, ln_ref, wattn_ref, w2_ref, hT_ref, qkv_ref, w1f_ref,
             xg, lng, watt, zsend, zrecv, zq, s1, s2,
             xsend, xrecv, lsend, lrecv, asend, arecv, zsend_sem, zrecv_sem, qsend, qrecv, wsend, wrecv):
    z, p, core, partner, xn, yn, diag, zs = coords()
    xg[z, p] = xT_ref[...]
    lng[z, p] = ln_ref[...]
    entry_barrier(z, p, zs)
    sends = []

    def send(sem_i, src_z, src_p, dev):
        c = rcopy(xg.at[src_z, src_p], xg.at[src_z, src_p], xsend.at[sem_i], xrecv.at[src_z, src_p], dev)
        c.start()
        sends.append(c)

    def lsendf(sem_i, src_z, src_p, dev):
        c = rcopy(lng.at[src_z, src_p], lng.at[src_z, src_p], lsend.at[sem_i], lrecv.at[src_z, src_p], dev)
        c.start()
        sends.append(c)

    def wait_x(src_z, src_p):
        rcopy(xg.at[src_z, src_p], xg.at[src_z, src_p], xsend.at[0], xrecv.at[src_z, src_p], (z, p)).wait_recv()

    def wait_l(src_z, src_p):
        rcopy(lng.at[src_z, src_p], lng.at[src_z, src_p], lsend.at[0], lrecv.at[src_z, src_p], (z, p)).wait_recv()

    half = C1 // 2

    def w_piece(i, src, dst, k, dev):
        return rcopy(
            w2_ref.at[:, pl.ds(pl.multiple_of(dst * 256 + i * half, 16), half), :],
            w1f_ref.at[src, :, pl.ds(i * half, half), :],
            wsend.at[i, k], wrecv.at[i, src], dev)

    def send_w(i):
        for k in (3, 2, 1):
            c = w_piece(i, z, zs[k], k, (zs[k], p))
            c.start()
            sends.append(c)

    n = 0
    ln = 0
    for k in (3, 2, 1):
        send(n, z, p, (zs[k], p))
        lsendf(ln, z, p, (zs[k], p))
        n += 1
        ln += 1
    for dev in (xn, yn, partner):
        send(n, z, p, (z, dev))
        n += 1
    for k in (3, 2, 1):
        c = rcopy(wattn_ref.at[pl.ds(attn_start(zs[k]), 80), :], watt.at[z], asend.at[k], arecv.at[z], (zs[k], p))
        c.start()
        sends.append(c)
    send_w(0)
    watt[z] = wattn_ref[pl.ds(attn_start(z), 80), :]
    for j in range(1, NP):
        lsendf(ln, z, p, (z, (p + j) % NP))
        ln += 1
    for k in range(1, NZ):
        wait_x(zs[k], p)
        for dev in (xn, yn, partner):
            send(n, zs[k], p, (z, dev))
            n += 1
        wait_l(zs[k], p)
        for j in range(1, NP):
            lsendf(ln, zs[k], p, (z, (p + j) % NP))
            ln += 1
    for k in range(NZ):
        wait_x(zs[k], xn)
        if k % 2:
            send(n, zs[k], xn, (z, yn))
            n += 1
        send(n, zs[k], xn, (z, partner))
        n += 1
        wait_x(zs[k], yn)
        if k % 2 == 0:
            send(n, zs[k], yn, (z, xn))
            n += 1
        send(n, zs[k], yn, (z, partner))
        n += 1
    for k in range(NZ):
        wait_x(zs[k], diag)
        send(n, zs[k], diag, (z, partner))
        n += 1
    pd = [partner + xn - p, partner + yn - p, partner + diag - p]
    for k in range(NZ):
        wait_x(zs[k], partner)
    for k in range(NZ):
        for q in pd:
            wait_x(zs[k], q)
    for k in range(NZ):
        for j in range(1, NP):
            wait_l(zs[k], (p + j) % NP)

    s1[...] = jnp.zeros_like(s1)
    s2[...] = jnp.zeros_like(s2)

    def stat(i, carry):
        blk = xg[i // NP, i % NP].astype(F32).reshape(8, 8, 512)
        s1[...] += jnp.sum(blk, axis=0)
        s2[...] += jnp.sum(blk * blk, axis=0)
        return carry

    lax.fori_loop(0, NZ * NP, stat, 0)
    mean = jnp.sum(s1[...], axis=0, keepdims=True) / 2048.0
    var = jnp.sum(s2[...], axis=0, keepdims=True) / 2048.0 - mean * mean
    rstd = lax.rsqrt(var + LN_EPS)
    lnT = jnp.concatenate([lng[i // NP, i % NP, 0:1, :] for i in range(32)] + [jnp.zeros((96, 128), F32)], axis=0).T
    for i in range(NZ * NP):
        sc = lnT[0:64, i:i + 1]
        hT_ref[i * 64:(i + 1) * 64, :] = ((xg[i // NP, i % NP].astype(F32) - mean) * rstd * sc).astype(BF16)

    for k in range(1, NZ):
        rcopy(watt.at[z], watt.at[zs[k]], asend.at[0], arecv.at[zs[k]], (z, p)).wait_recv()
    part = None
    for q in range(NZ):
        t = jnp.dot(watt[q], hT_ref[q * 512:(q + 1) * 512, :], preferred_element_type=F32)
        part = t if part is None else part + t
    part = part.astype(BF16)
    for q in range(NZ):
        zsend[q] = part[:, q * 128:(q + 1) * 128]
    for k in (3, 2, 1):
        c = rcopy(zsend.at[zs[k]], zrecv.at[z], zsend_sem.at[k], zrecv_sem.at[z], (zs[k], p))
        c.start()
        sends.append(c)
    send_w(1)
    zrecv[z] = zsend[z]
    for k in range(1, NZ):
        rcopy(zsend.at[0], zrecv.at[zs[k]], zsend_sem.at[0], zrecv_sem.at[zs[k]], (z, p)).wait_recv()
    zt = jnp.concatenate([zrecv[0].astype(F32), zrecv[1].astype(F32)[16:80], zrecv[2].astype(F32), zrecv[3].astype(F32)[16:80]], axis=0)
    zq[...] = zt.T.astype(BF16).reshape(NP, 16, 288)
    for j in range(1, NP):
        q = (p + j) % NP
        c = rcopy(zq.at[q], qkv_ref.at[p], qsend.at[j], qrecv.at[p], (z, q))
        c.start()
        sends.append(c)
    qkv_ref[p] = zq[p]
    for j in range(1, NP):
        q = (p + j) % NP
        rcopy(zq.at[0], qkv_ref.at[q], qsend.at[0], qrecv.at[q], (z, p)).wait_recv()
    for i in range(2):
        for k in range(1, NZ):
            w_piece(i, zs[k], z, 0, (z, p)).wait_recv()
    for c in sends:
        c.wait_send()


def call_a(xT, lnb, wattnT, w2):
    vm = pl.BlockSpec(memory_space=pltpu.VMEM)
    hbm = pl.BlockSpec(memory_space=pl.ANY)
    return pl.pallas_call(
        kernel_a,
        out_shape=(
            jax.ShapeDtypeStruct((2048, 512), BF16),
            jax.ShapeDtypeStruct((NP, 16, 288), BF16),
            jax.ShapeDtypeStruct((NZ, 2, C1, 512), BF16),
        ),
        in_specs=[vm] * 3 + [hbm],
        out_specs=(vm, vm, hbm),
        scratch_shapes=[
            pltpu.VMEM((NZ, NP, 64, 512), BF16),
            pltpu.VMEM((NZ, NP, 8, 128), F32),
            pltpu.VMEM((NZ, 80, 512), BF16),
            pltpu.VMEM((NZ, 80, 128), BF16),
            pltpu.VMEM((NZ, 80, 128), BF16),
            pltpu.VMEM((NP, 16, 288), BF16),
            pltpu.VMEM((8, 512), F32),
            pltpu.VMEM((8, 512), F32),
            pltpu.SemaphoreType.DMA((40,)),
            pltpu.SemaphoreType.DMA((NZ, NP)),
            pltpu.SemaphoreType.DMA((40,)),
            pltpu.SemaphoreType.DMA((NZ, NP)),
            pltpu.SemaphoreType.DMA((NZ,)),
            pltpu.SemaphoreType.DMA((NZ,)),
            pltpu.SemaphoreType.DMA((NZ,)),
            pltpu.SemaphoreType.DMA((NZ,)),
            pltpu.SemaphoreType.DMA((NP,)),
            pltpu.SemaphoreType.DMA((NP,)),
            pltpu.SemaphoreType.DMA((2, NZ)),
            pltpu.SemaphoreType.DMA((2, NZ)),
        ],
        compiler_params=pltpu.CompilerParams(collective_id=0, has_side_effects=True, vmem_limit_bytes=56 * 1024 * 1024),
        name='gather_norm_qkv',
    )(xT, lnb, wattnT, w2)


def kernel_b(len_ref, q_ref, k_ref, v_ref, kc_ref, vc_ref, o_ref, kn_ref, vn_ref, kbuf, vbuf, isem, osem):
    rows = kbuf.shape[0]
    seq = kbuf.shape[1]

    def load(b, t):
        return pltpu.make_async_copy((kc_ref, vc_ref)[t].at[b], (kbuf, vbuf)[t].at[b], isem.at[b, t])

    def store(b, t):
        return pltpu.make_async_copy((kbuf, vbuf)[t].at[b], (kn_ref, vn_ref)[t].at[b], osem.at[b, t])

    for b in range(rows):
        load(b, 0).start()
        load(b, 1).start()

    def insert(buf, b, length, new):
        base = pl.multiple_of((length // 16) * 16, 16)
        hit = base + lax.broadcasted_iota(jnp.int32, (16, 128), 0) == length
        buf[b, pl.ds(base, 16), :] = jnp.where(hit, new.astype(F32), buf[b, pl.ds(base, 16), :].astype(F32)).astype(BF16)

    def attend(b, length, n):
        scores = lax.dot_general(q_ref[b], kbuf[b, 0:n, :], (((1,), (1,)), ((), ())), preferred_element_type=F32) * (128.0 ** -0.5)
        slot = lax.broadcasted_iota(jnp.int32, scores.shape, 1)
        scores = jnp.where(slot <= length, scores, -1e30)
        top = jnp.max(scores, axis=1, keepdims=True)
        e = jnp.exp(scores - top)
        probs = (e / jnp.sum(e, axis=1, keepdims=True)).astype(BF16)
        return jnp.dot(probs, vbuf[b, 0:n, :], preferred_element_type=F32).astype(BF16)

    def pair(i, carry):
        b0 = 2 * i
        b1 = 2 * i + 1
        l0 = len_ref[b0]
        l1 = len_ref[b1]
        for b, length in ((b0, l0), (b1, l1)):
            load(b, 0).wait()
            load(b, 1).wait()
            insert(kbuf, b, length, k_ref[b])
            insert(vbuf, b, length, v_ref[b])
        last = jnp.maximum(l0, l1) // 512
        for t in range(seq // 512):
            @pl.when(last == t)
            def _():
                n = 512 * (t + 1)
                r0 = attend(b0, l0, n)
                r1 = attend(b1, l1, n)
                o_ref[b0] = r0
                o_ref[b1] = r1
        for b in (b0, b1):
            store(b, 0).start()
            store(b, 1).start()
        return carry

    lax.fori_loop(0, rows // 2, pair, 0)
    for b in range(rows):
        store(b, 0).wait()
        store(b, 1).wait()


def call_b(lengths, q_rot, k_rot, v_tok, k_cache, v_cache):
    rows, seq, hd = k_cache.shape
    heads = q_rot.shape[1]
    vm = pl.BlockSpec(memory_space=pltpu.VMEM)
    hbm = pl.BlockSpec(memory_space=pl.ANY)
    return pl.pallas_call(
        kernel_b,
        in_specs=[pl.BlockSpec(memory_space=pltpu.SMEM), vm, vm, vm, hbm, hbm],
        out_specs=(vm, hbm, hbm),
        out_shape=(
            jax.ShapeDtypeStruct((rows, heads, hd), BF16),
            jax.ShapeDtypeStruct(k_cache.shape, BF16),
            jax.ShapeDtypeStruct(v_cache.shape, BF16),
        ),
        scratch_shapes=[
            pltpu.VMEM((rows, seq, hd), BF16),
            pltpu.VMEM((rows, seq, hd), BF16),
            pltpu.SemaphoreType.DMA((rows, 2)),
            pltpu.SemaphoreType.DMA((rows, 2)),
        ],
        compiler_params=pltpu.CompilerParams(vmem_limit_bytes=58 * 1024 * 1024),
        cost_estimate=pl.CostEstimate(flops=12_000_000_000, bytes_accessed=33_000_000, transcendentals=0),
        name='attend',
    )(lengths, q_rot, k_rot, v_tok, k_cache, v_cache)


def kernel_c(hT_hbm, w2_ref, w1f_ref, p1_ref, p2_ref, p3_ref, wd_hbm, wo_hbm, o_ref, xT_ref, y_ref,
             hT, wvA, wvB, wd, wo, wdAT, wdBT, woT, og, hidA, hidB, yA, ysum, r1, acc, r2,
             lsem, wsem, wbsend, wbrecv, osend, orecv, gsend, grecv, hasend, harecv, hbsend, hbrecv,
             r1send, r1recv, r2send, r2recv):
    z, p, core, partner, xn, yn, diag, zs = coords()
    local = [pltpu.make_async_copy(hT_hbm, hT, lsem.at[0])]
    local.append(pltpu.make_async_copy(w2_ref.at[:, pl.ds(pl.multiple_of(z * 256, 256), CA), :], wvA.at[z], wsem.at[0]))
    for s, p_ref in ((1, p1_ref), (2, p2_ref), (3, p3_ref)):
        src = (z + NZ - s) % NZ
        local.append(pltpu.make_async_copy(w1f_ref.at[src], wvA.at[src, :, pl.ds(0, C1), :], wsem.at[2 * s]))
        local.append(pltpu.make_async_copy(p_ref, wvA.at[src, :, pl.ds(C1, C2), :], wsem.at[2 * s + 1]))
    late = [
        pltpu.make_async_copy(w2_ref.at[:, pl.ds(pl.multiple_of(z * 256 + CA, 32), C3), :], wvB.at[z], wsem.at[1]),
        pltpu.make_async_copy(wd_hbm, wd, lsem.at[1]),
        pltpu.make_async_copy(wo_hbm, wo, lsem.at[2]),
    ]
    for c in local + late:
        c.start()
    entry_barrier(z, p, zs)
    sends = []

    def w_piece(src, dst, k, dev):
        return rcopy(w2_ref.at[:, pl.ds(pl.multiple_of(dst * 256 + CA, 32), C3), :], wvB.at[src], wbsend.at[k], wbrecv.at[src], dev)

    for k in (3, 2, 1):
        c = w_piece(z, zs[k], k, (zs[k], p))
        c.start()
        sends.append(c)
    for j in range(1, NP):
        q = (p + j) % NP
        c = rcopy(o_ref.at[q], og.at[z, p], osend.at[j], orecv.at[p], (z, q))
        c.start()
        sends.append(c)
    og[z, p] = o_ref[p]

    def gated(wv, n):
        g = None
        for q in range(NZ):
            t = jnp.dot(wv[q].reshape(2 * n, 512), hT[q * 512:(q + 1) * 512, :], preferred_element_type=F32)
            g = t if g is None else g + t
        gate = g[0:n].astype(BF16).astype(F32)
        up = g[n:2 * n].astype(BF16).astype(F32)
        return (jax.nn.silu(gate) * up).astype(BF16)

    def fwd_a(sem, src, dev):
        return rcopy(hidA.at[src], hidA.at[src], hasend.at[sem], harecv.at[src], dev)

    def fwd_b(sem, src, ch, dev):
        return rcopy(hidB.at[ch, src], hidB.at[ch, src], hbsend.at[sem, ch], hbrecv.at[src, ch], dev)

    for c in local:
        c.wait()
    hidA[z] = gated(wvA, CA)

    @pl.when(z < 3)
    def _():
        fwd_a(0, z, (z + 1, p)).start()

    @pl.when(z > 0)
    def _():
        fwd_a(1, z, (z - 1, p)).start()

    for j in range(1, NP):
        q = (p + j) % NP
        rcopy(o_ref.at[0], og.at[z, q], osend.at[0], orecv.at[q], (z, p)).wait_recv()
    for k in (3, 2, 1):
        c = rcopy(og.at[z], og.at[z], gsend.at[k], grecv.at[z], (zs[k], p))
        c.start()
        sends.append(c)
    for c in late:
        c.wait()
    wdAT[...] = jnp.concatenate([wd[q * 256:q * 256 + CA, :] for q in range(NZ)], axis=0).T
    wdBT[...] = jnp.concatenate([wd[q * 256 + CA:(q + 1) * 256, :] for q in range(NZ)], axis=0).T
    woT[...] = wo[...].T

    def pass_a(k):
        @pl.when(z >= k)
        def _():
            fwd_a(0, z - k, (z, p)).wait_recv()

            @pl.when(z < 3)
            def _():
                fwd_a(2 * k, z - k, (z + 1, p)).start()

        @pl.when(z + k <= 3)
        def _():
            fwd_a(0, z + k, (z, p)).wait_recv()

            @pl.when(z > 0)
            def _():
                fwd_a(2 * k + 1, z + k, (z - 1, p)).start()

    for k in range(1, NZ):
        w_piece(zs[k], z, 0, (z, p)).wait_recv()
    hb = gated(wvB, C3)
    for ch in range(CHUNKS):
        hidB[ch, z] = hb[:, ch * LANES:(ch + 1) * LANES]
    pass_a(1)

    @pl.when(z < 3)
    def _():
        for ch in range(CHUNKS):
            fwd_b(0, z, ch, (z + 1, p)).start()

    @pl.when(z > 0)
    def _():
        for ch in range(CHUNKS):
            fwd_b(1, z, ch, (z - 1, p)).start()

    pass_a(2)
    pass_a(3)

    def pass_b(k, ch):
        @pl.when(z >= k)
        def _():
            fwd_b(0, z - k, ch, (z, p)).wait_recv()

            @pl.when(z < 3)
            def _():
                fwd_b(2 * k, z - k, ch, (z + 1, p)).start()

        @pl.when(z + k <= 3)
        def _():
            fwd_b(0, z + k, ch, (z, p)).wait_recv()

            @pl.when(z > 0)
            def _():
                fwd_b(2 * k + 1, z + k, ch, (z - 1, p)).start()

    for ch in range(CHUNKS):
        pass_b(1, ch)
    for k in range(1, NZ):
        rcopy(og.at[0], og.at[zs[k]], gsend.at[0], grecv.at[zs[k]], (z, p)).wait_recv()
    yA[...] = jnp.dot(wdAT[...], hidA[...].reshape(NZ * CA, 512), preferred_element_type=F32) + lax.dot_general(
        woT[...], og[...].reshape(512, 256), (((1,), (1,)), ((), ())), preferred_element_type=F32)
    for ch in range(CHUNKS):
        pass_b(2, ch)

    chip = p // 2
    others = [xn // 2, yn // 2, diag // 2]

    def d2d(ch):
        return rcopy(ysum.at[ch, 1 - core], r1.at[ch], r1send.at[ch], r1recv.at[ch], (z, partner))

    def hop(ch, i, dev):
        return rcopy(acc.at[ch, i], r2.at[ch, i], r2send.at[ch, i], r2recv.at[ch, i], (z, dev))

    def stage1(ch):
        pass_b(3, ch)
        lanes = slice(ch * LANES, (ch + 1) * LANES)
        yt = yA[:, lanes] + jnp.dot(wdBT[...], hidB[ch].reshape(NZ * C3, LANES), preferred_element_type=F32)
        yt = yt.reshape(4, 2, 64, LANES)
        for i in range(4):
            for j in range(2):
                ysum[ch, j, i] = yt[i, j]
        d2d(ch).start()

    def stage2(ch):
        d2d(ch).wait_recv()
        for i, (t, dev) in enumerate(zip(others, (xn, yn, diag))):
            acc[ch, i] = ysum[ch, core, t] + r1[ch, t]
            hop(ch, i, dev).start()

    def stage3(ch):
        lanes = slice(ch * LANES, (ch + 1) * LANES)
        mine = ysum[ch, core, chip] + r1[ch, chip]
        for i, dev in enumerate((xn, yn, diag)):
            hop(ch, i, dev).wait_recv()
            mine = mine + r2[ch, i]
        y_ref[:, lanes] = (xT_ref[:, lanes].astype(F32) + mine).astype(BF16)

    for t in range(CHUNKS + 2):
        if t < CHUNKS:
            stage1(t)
        if 1 <= t <= CHUNKS:
            stage2(t - 1)
        if t >= 2:
            stage3(t - 2)

    for c in sends:
        c.wait_send()
    for ch in range(CHUNKS):
        d2d(ch).wait_send()
        for i, dev in enumerate((xn, yn, diag)):
            hop(ch, i, dev).wait_send()
    for k in range(NZ - 1):
        @pl.when((z >= k) & (z < 3))
        def _():
            fwd_a(2 * k, z, (z, p)).wait_send()
            for ch in range(CHUNKS):
                fwd_b(2 * k, z, ch, (z, p)).wait_send()

        @pl.when((z + k <= 3) & (z > 0))
        def _():
            fwd_a(2 * k + 1, z, (z, p)).wait_send()
            for ch in range(CHUNKS):
                fwd_b(2 * k + 1, z, ch, (z, p)).wait_send()


def call_c(hT, w2, w1f, ps, wd, wo, o8, xT):
    vm = pl.BlockSpec(memory_space=pltpu.VMEM)
    hbm = pl.BlockSpec(memory_space=pl.ANY)
    return pl.pallas_call(
        kernel_c,
        out_shape=jax.ShapeDtypeStruct((64, 512), BF16),
        in_specs=[hbm] * 8 + [vm, vm],
        out_specs=vm,
        scratch_shapes=[
            pltpu.VMEM((2048, 512), BF16),
            pltpu.VMEM((NZ, 2, CA, 512), BF16),
            pltpu.VMEM((NZ, 2, C3, 512), BF16),
            pltpu.VMEM((1024, 512), BF16),
            pltpu.VMEM((256, 512), BF16),
            pltpu.VMEM((512, NZ * CA), BF16),
            pltpu.VMEM((512, NZ * C3), BF16),
            pltpu.VMEM((512, 256), BF16),
            pltpu.VMEM((NZ, NP, 16, 256), BF16),
            pltpu.VMEM((NZ, CA, 512), BF16),
            pltpu.VMEM((CHUNKS, NZ, C3, LANES), BF16),
            pltpu.VMEM((512, 512), F32),
            pltpu.VMEM((CHUNKS, 2, 4, 64, LANES), F32),
            pltpu.VMEM((CHUNKS, 4, 64, LANES), F32),
            pltpu.VMEM((CHUNKS, 3, 64, LANES), F32),
            pltpu.VMEM((CHUNKS, 3, 64, LANES), F32),
            pltpu.SemaphoreType.DMA((3,)),
            pltpu.SemaphoreType.DMA((8,)),
            pltpu.SemaphoreType.DMA((NZ,)),
            pltpu.SemaphoreType.DMA((NZ,)),
            pltpu.SemaphoreType.DMA((NP,)),
            pltpu.SemaphoreType.DMA((NP,)),
            pltpu.SemaphoreType.DMA((NZ,)),
            pltpu.SemaphoreType.DMA((NZ,)),
            pltpu.SemaphoreType.DMA((8,)),
            pltpu.SemaphoreType.DMA((NZ,)),
            pltpu.SemaphoreType.DMA((8, CHUNKS)),
            pltpu.SemaphoreType.DMA((NZ, CHUNKS)),
            pltpu.SemaphoreType.DMA((CHUNKS,)),
            pltpu.SemaphoreType.DMA((CHUNKS,)),
            pltpu.SemaphoreType.DMA((CHUNKS, 3)),
            pltpu.SemaphoreType.DMA((CHUNKS, 3)),
        ],
        compiler_params=pltpu.CompilerParams(collective_id=1, has_side_effects=True, vmem_limit_bytes=58 * 1024 * 1024),
        cost_estimate=pl.CostEstimate(flops=12_000_000_000, bytes_accessed=6_000_000, transcendentals=0),
        name='mlp_out',
    )(hT, w2, w1f, *ps, wd, wo, o8, xT)


def solution(mesh):
    all_axes = ('x', 'yz')

    def local_step(x_in, ln_scale, w_gate_up, w_attn, w_down, w_out, k_cache, v_cache, lengths, positions):
        z = lax.axis_index('x')
        xT = x_in.T
        wattnT = w_attn.T
        lnb = jnp.broadcast_to(jnp.pad(ln_scale, (0, 64))[None, :], (8, 128))
        w2 = jnp.transpose(w_gate_up, (1, 2, 0))
        hT, qkv, w1f = call_a(xT, lnb, wattnT, w2)
        w2b, hT, qkv, w1f = lax.optimization_barrier((w2, hT, qkv, w1f))
        ps = []
        for s in range(1, NZ):
            piece = lax.dynamic_slice(w2b, (0, ((z + s) % NZ) * 256 + C1, 0), (2, C2, 512))
            ps.append(lax.ppermute(piece, 'x', [(i, (i + s) % NZ) for i in range(NZ)]))
        proj = jnp.transpose(qkv, (1, 0, 2)).reshape(16, 2304)
        q_raw = proj[:, :2048].reshape(16, 16, 128)
        k_tok = proj[:, 2048:2176]
        v_tok = proj[:, 2176:]
        q_rot = rotary(q_raw.astype(F32), positions).astype(BF16)
        k_rot = rotary(k_tok[:, None, :].astype(F32), positions).astype(BF16)
        o, k_new, v_new = call_b(lengths, q_rot, k_rot, v_tok[:, None, :], k_cache, v_cache)
        o8 = jnp.transpose(o.reshape(16, NP, 256), (1, 0, 2))
        yT = call_c(hT, w2b, w1f, ps, w_down, w_out, o8, xT)
        return yT.T, k_new, v_new

    row_spec = P(None, all_axes)
    vec_spec = P(all_axes)
    cache_spec = P(all_axes, None, None)
    return jax.shard_map(
        local_step,
        mesh=mesh,
        in_specs=(row_spec, vec_spec, P('x', None, 'yz'), P('x', 'yz'), P('yz', 'x'), P('yz', 'x'), cache_spec, cache_spec, vec_spec, vec_spec),
        out_specs=(row_spec, cache_spec, cache_spec),
        check_vma=False,
    )
```

time: 145 us -> 130 us (0.90)
  waiting for transfers between devices: 19.6 us -> 0.01 us
  Pallas kernels: 106 us -> 109 us
  starting transfers between devices: 2.03 us -> 4.06 us
    ppermute x3, waiting for transfers between devices: 19.6 us -> 0.01 us  [local_step(): ps.append(lax.ppermute(piece, 'x', [(i, (i + s) % NZ) for i in range(NZ)]))]
    pallas_call x1, Pallas kernels: 41.6 us -> 55.8 us  [call_c(): pl.pallas_call(kernel_c, out_shape=jax.ShapeDtypeStruct((64, 512), BF16),...]
    pallas_call x1, Pallas kernels: 44.9 us -> 38.7 us  [call_a(): pl.pallas_call(kernel_a, out_shape=(jax.ShapeDtypeStruct((2048, 512), BF1...]
    unnamed x14 -> x11, local copies, waits for them, and re-layouts: 2.86 us -> 8.44 us
    pallas_call x1, Pallas kernels: 19.7 us -> 14.4 us  [call_b(): pl.pallas_call(kernel_b, in_specs=[pl.BlockSpec(memory_space=pltpu.SMEM),...]
    reshape x1 -> x0, local copies, waits for them, and re-layouts: 3.15 us -> none  [local_step(): w_gate_up.reshape(512, 2, NZ, 256)]
    transpose x1 -> x0, local copies, waits for them, and re-layouts: 3 us -> none  [local_step(): jnp.transpose(w_gate_up.reshape(512, 2, NZ, 256), (2, 1, 3, 0))]
    squeeze x1 -> x0, local copies, waits for them, and re-layouts: 2.71 us -> none  [local_step(): piece = lax.dynamic_index_in_dim(w4, (z + s) % NZ, 0, keepdims=False)]
  transfers between devices with their start and end apart: 3 -> 3, of which waited for: 1 -> 0; matrix products, arithmetic and copies ran while one was open for 3% -> 4% of each run, Pallas kernels for 14% -> 11%
where the time goes in v2:
time: 130 us
  Pallas kernels  109 us (84%)
  local copies, waits for them, and re-layouts  14.1 us (11%)
  starting transfers between devices  4.06 us (3%)
  other arithmetic  1.93 us (1%)
    pallas_call x1, Pallas kernels, call_c(): pl.pallas_call(kernel_c, out_shape=jax.ShapeDtypeStruct((64, 512), BF16),...  55.8 us
    pallas_call x1, Pallas kernels, call_a(): pl.pallas_call(kernel_a, out_shape=(jax.ShapeDtypeStruct((2048, 512), BF1...  38.7 us
    pallas_call x1, Pallas kernels, call_b(): pl.pallas_call(kernel_b, in_specs=[pl.BlockSpec(memory_space=pltpu.SMEM),...  14.4 us
    unnamed x11, local copies, waits for them, and re-layouts  8.44 us
    ppermute x3, starting transfers between devices, local_step(): ps.append(lax.ppermute(piece, 'x', [(i, (i + s) % NZ) for i in range(NZ)]))  4.06 us
  transfers between devices with their start and end apart: 3, of which 0 were waited for; matrix products, arithmetic and copies ran while one was open for 4% of the time, Pallas kernels for 11%

profile of v2, /device:TPU:0, one launch (start us, length us, event | category | flops | bytes accessed | tf_op | source)
XLA Modules:
  0.0 129.9 jit_solution(17602662070023303876)
XLA Ops:
  0.7 6.1 %copy.20 = bf16[512,2,1024]{0,2,1:T(8,128)(2,1)} copy(bf16[512,2,1024]{2,1,0:T(2,128)(2,1)} %param.12) | data formatting | bytes 4194304 | tf_op args[2]
  6.8 0.7 pad.4
  7.5 0.6 broadcast_in_dim.4.ln_ref
  8.1 38.7 %gather_norm_qkv.1 = (bf16[2048,512]{1,0:T(8,128)(2,1)}, bf16[8,16,288]{2,1,0:T(8,128)(2,1)}, bf16[4,2,64,512]{3,2,1,0:T(8,128)(2,1)}) custom-call(bf16[64,512]{1,0:T(8,128)(2,1)} %bitcast.22, f32[8,128]{1,0:T(8,128)} %broadcast_in_dim.4.ln_ref, bf16[288,512]{1,0:T(8,128)(2,1)} %bitcast.19, bf16[2,1024,512]{2,1,0:T(8,128)(2,1)} %bitcast.15), custom_call_target="tpu_custom_call" | custom-call | tf_op jit(solution)/shard_map/gather_norm_qkv/pallas_call | solution.py:220
  46.8 1.2 constant_dynamic-slice_fusion
  47.9 2.1 %collective-permute-start.2 = (bf16[2,96,512]{2,1,0:T(8,128)(2,1)S(1)}, bf16[2,96,512]{2,1,0:T(8,128)(2,1)S(1)}, u32[]{:S(2)}, u32[]{:S(2)}) collective-permute-start(bf16[2,96,512]{2,1,0:T(8,128)(2,1)S(1)} %get-tuple-element.23), channel_id=1, source_target_pairs={{0,24},{8,0},{16,8},{24,16},{1,25},{9,1},{17,9},{25,17},{2,26},{10... | collective-permute-start | bytes 589832 | tf_op jit(solution)/shard_map/ppermute | solution.py:601
  50.0 0.4 collective-permute-start.1
  50.4 1.6 %collective-permute-start = (bf16[2,96,512]{2,1,0:T(8,128)(2,1)S(1)}, bf16[2,96,512]{2,1,0:T(8,128)(2,1)S(1)}, u32[]{:S(2)}, u32[]{:S(2)}) collective-permute-start(bf16[2,96,512]{2,1,0:T(8,128)(2,1)S(1)} %get-tuple-element.25), channel_id=1, source_target_pairs={{0,8},{8,16},{16,24},{24,0},{1,9},{9,17},{17,25},{25,1},{2,10},{10... | collective-permute-start | bytes 589832 | tf_op jit(solution)/shard_map/ppermute | solution.py:601
  52.0 0.9 copy.21
  52.9 0.1 reshape.152
  53.1 0.6 copy.23.v_ref
  53.7 0.1 multiply_cosine_fusion
  53.9 0.1 mul.101
  53.9 0.3 subtract_convert_fusion.1
  54.2 0.7 pad_maximum_fusion.1.k_ref
  54.9 0.1 subtract_convert_fusion
  55.0 0.7 pad_maximum_fusion.q_ref
  55.7 14.4 %attend.1 = (bf16[16,16,128]{2,1,0:T(8,128)(2,1)}, bf16[16,2048,128]{2,1,0:T(8,128)(2,1)}, bf16[16,2048,128]{2,1,0:T(8,128)(2,1)}) custom-call(s32[16]{0:T(128)} %len_ref.1, bf16[16,16,128]{2,1,0:T(8,128)(2,1)} %pad_maximum_fusion.q_ref, bf16[16,1,128]{2,1,0:T(2,128)(2,1)} %pad_maximum_fusion.1.k_ref, bf16[16,1,128]{2,1,0:T(2,128)(2,1)} %copy.23.v_ref, ...), custom_call_target="tpu_custom_call" | custom-call | flops 12000000000 | bytes 33000000 | tf_op jit(solution)/shard_map/attend/pallas_call | solution.py:319
  70.2 0.9 reshape.153
  71.0 0.6 copy.27
  71.7 0.6 copy-done
  72.4 0.1 copy-done.1
  72.5 55.8 %mlp_out.1 = bf16[64,512]{1,0:T(8,128)(2,1)} custom-call(bf16[2048,512]{1,0:T(8,128)(2,1)} %get-tuple-element.16.hT_hbm, bf16[2,1024,512]{2,1,0:T(8,128)(2,1)} %bitcast.17, bf16[4,2,64,512]{3,2,1,0:T(8,128)(2,1)} %get-tuple-element.18.w1f_ref, bf16[2,96,512]{2,1,0:T(8,128)(2,1)} %copy-done.2, bf16[2,96,512]{2,1,0:T(8,128)(2,1)} %copy-done.1, ...), custom_call_target="tpu_custom_call" | custom-call | flops 12000000000 | bytes 6000000 | tf_op jit(solution)/shard_map/mlp_out/pallas_call | solution.py:542
  128.4 1.5 %copy.29 = bf16[512,64]{0,1:T(8,128)(2,1)} copy(bf16[512,64]{0,1:T(8,128)(2,1)} %bitcast.25) | data formatting | bytes 131072
  (14 shorter events, 0.1 us)
Async XLA Ops:
  0.6 52.5 %copy-start.3 = (s32[16]{0:T(128)S(1)}, s32[16]{0:T(128)}, u32[]{:S(2)}) copy-start(s32[16]{0:T(128)} %param.19) | copy-start | bytes 196
  47.9 23.7 %collective-permute-start.2 = (bf16[2,96,512]{2,1,0:T(8,128)(2,1)S(1)}, bf16[2,96,512]{2,1,0:T(8,128)(2,1)S(1)}, u32[]{:S(2)}, u32[]{:S(2)}) collective-permute-start(bf16[2,96,512]{2,1,0:T(8,128)(2,1)S(1)} %get-tuple-element.23), channel_id=1, source_target_pairs={{0,24},{8,0},{16,8},{24,16},{1,25},{9,1},{17,9},{25,17},{2,26},{10... | collective-permute-start | bytes 589832 | tf_op jit(solution)/shard_map/ppermute | solution.py:601
  50.0 21.7 %collective-permute-start.1 = (bf16[2,96,512]{2,1,0:T(8,128)(2,1)S(1)}, bf16[2,96,512]{2,1,0:T(8,128)(2,1)S(1)}, u32[]{:S(2)}, u32[]{:S(2)}) collective-permute-start(bf16[2,96,512]{2,1,0:T(8,128)(2,1)S(1)} %get-tuple-element.24), channel_id=1, source_target_pairs={{0,16},{8,24},{16,0},{24,8},{1,17},{9,25},{17,1},{25,9},{2,18},{10... | collective-permute-start | bytes 589832 | tf_op jit(solution)/shard_map/ppermute | solution.py:601
  50.4 21.3 %collective-permute-start = (bf16[2,96,512]{2,1,0:T(8,128)(2,1)S(1)}, bf16[2,96,512]{2,1,0:T(8,128)(2,1)S(1)}, u32[]{:S(2)}, u32[]{:S(2)}) collective-permute-start(bf16[2,96,512]{2,1,0:T(8,128)(2,1)S(1)} %get-tuple-element.25), channel_id=1, source_target_pairs={{0,8},{8,16},{16,24},{24,0},{1,9},{9,17},{17,25},{25,1},{2,10},{10... | collective-permute-start | bytes 589832 | tf_op jit(solution)/shard_map/ppermute | solution.py:601
  71.7 0.7 copy-start
  71.7 0.8 copy-start.1
  71.7 0.8 copy-start.2
